TPU v7x, 32 devices: a whole 2x2x4 slice. The times are simulated.
32 devices in a mesh: ctx: 8 (over z, core), tp: 4 (over y, x).
Axes of the slice: x: 2, y: 2, z: 4, core: 2. Of those that a mesh axis runs over, the one named last changes fastest.
Arguments:
- act_codes: bfloat16 [2048, 4096], P(('ctx', 'tp')), may hold values from -6 to 6
- scale_exps: int32 [2048, 32], P(('ctx', 'tp')), may hold values from -2 to 2
- weight: bfloat16 [4096, 6144], P(None, 'tp'), may hold values from -0.09375 to 0.09375
- grad_out: bfloat16 [2048, 6144], P('ctx', 'tp'), may hold values from -6 to 6
Outputs:
- grad_input: bfloat16 [2048, 4096], P(('ctx', 'tp'))
- grad_weight: float32 [4096, 6144], P('ctx', 'tp')
All inputs are finite; a program needn't handle non-finite values.
Results may differ from a plain program's by a relative error of at most 0.023.
Values may be sent and summed in bfloat16 or wider, within the bound.
A program may use at most 64 MiB of HBM per device.

v0:
```python
import functools

import jax
import jax.numpy as jnp
from jax import lax
from jax.experimental import pallas as pl
from jax.experimental.pallas import tpu as pltpu
from jax.sharding import PartitionSpec as P

MESH = pl.DeviceIdType.MESH
CHUNKS = 4


def kernel(
    n_ctx, n_tp, tokens,
    codes_hbm, exps_hbm, weight_ref, grads_ref,
    gin_ref, gw_ref,
    codes_ref, exps_ref, w_buf, g_buf, a_send, a_buf, part, landed,
    in_sem, w_sem, g_sem,
    a_ssem, a_rsem, b_ssem, b_rsem, up_ssem, down_ssem, mate_ssem, g_rsem, p_ssem, p_rsem,
):
    n_line = n_ctx // 2
    me = lax.axis_index("ctx")
    tp = lax.axis_index("tp")
    core = lax.rem(me, 2)
    z = lax.div(me, 2)
    mate = me + 1 - 2 * core
    rows, width = codes_ref.shape
    block = width // exps_ref.shape[0]
    feats = width // n_ctx
    d_tile = w_buf.shape[1]
    n_d = w_buf.shape[0]
    scale = lax.rsqrt(jnp.float32(tokens))
    split = n_ctx * n_tp <= 64

    def load_w(i):
        return pltpu.make_async_copy(
            weight_ref.at[pl.ds(i * d_tile, d_tile)], w_buf.at[i], w_sem.at[i]
        )

    def load_g(k):
        size = g_buf.shape[2]
        return pltpu.make_async_copy(
            grads_ref.at[pl.ds(k * size, size)], g_buf.at[me, k], g_sem.at[k]
        )

    load_codes = pltpu.make_async_copy(codes_hbm, codes_ref, in_sem.at[0])
    load_exps = pltpu.make_async_copy(exps_hbm, exps_ref, in_sem.at[1])
    load_g(0).start()
    load_codes.start()
    load_exps.start()
    for k in range(1, CHUNKS):
        load_g(k).start()
    for i in range(n_d):
        load_w(i).start()

    barrier = pltpu.get_barrier_semaphore()
    for r in range(1, n_ctx):
        pl.semaphore_signal(
            barrier, inc=1, device_id=(lax.rem(me + r, n_ctx), tp), device_id_type=MESH
        )
    for r in range(1, n_tp):
        pl.semaphore_signal(
            barrier, inc=1, device_id=(me, lax.rem(tp + r, n_tp)), device_id_type=MESH
        )

    pl.semaphore_wait(barrier, n_ctx + n_tp - 2)

    def remote(src, dst, ssem, rsem, to):
        return pltpu.make_async_remote_copy(
            src_ref=src, dst_ref=dst, send_sem=ssem, recv_sem=rsem,
            device_id=to, device_id_type=MESH,
        )

    def act_copy(to):
        return remote(
            a_send.at[to], a_buf.at[me, tp], a_ssem.at[to], a_rsem.at[me], (to, tp)
        )

    def act_landing(source):
        return remote(
            a_send.at[source], a_buf.at[source, tp], a_ssem.at[source], a_rsem.at[source],
            (source, tp),
        )

    def spread_copy(s, q, src=None):
        return remote(
            a_buf.at[s, tp] if src is None else src,
            a_buf.at[s, tp], b_ssem.at[s, q], b_rsem.at[s, tp], (me, q),
        )

    def spread_landing(s, q):
        return remote(
            a_buf.at[s, q], a_buf.at[s, q], b_ssem.at[s, q], b_rsem.at[s, q], (me, q)
        )

    def spread_all(q):
        return remote(
            a_buf.at[:, tp], a_buf.at[:, tp], b_ssem.at[0, q], b_rsem.at[0, tp], (me, q)
        )

    def spread_all_landing(q):
        return remote(
            a_buf.at[:, q], a_buf.at[:, q], b_ssem.at[0, q], b_rsem.at[0, q], (me, q)
        )

    def pass_on(s, k, ssem, to):
        return remote(
            g_buf.at[s, k], g_buf.at[s, k], ssem.at[lax.div(s, 2), k], g_rsem.at[s, k], (to, tp)
        )

    def up(s, k):
        return pass_on(s, k, up_ssem, me + 2)

    def down(s, k):
        return pass_on(s, k, down_ssem, me - 2)

    def across(s, k):
        return pass_on(s, k, mate_ssem, mate)

    has_up = z < n_line - 1
    has_down = z > 0

    def send_own(k):
        load_g(k).wait()

        @pl.when(has_up)
        def _():
            up(me, k).start()

        @pl.when(has_down)
        def _():
            down(me, k).start()

        across(me, k).start()

    send_own(0)
    load_codes.wait()
    load_exps.wait()
    powers = jnp.exp2(exps_ref[...].astype(jnp.float32)).T
    for b in range(width // block):
        owner, place = divmod(b * block, feats)
        value = codes_ref[:, b * block : (b + 1) * block].astype(jnp.float32)
        value = value * powers[:, b : b + 1]
        a_send[owner, :, place : place + block] = value.astype(jnp.bfloat16)
    a_buf[me, tp] = a_send[me]
    for r in range(1, n_ctx):
        act_copy(lax.rem(me + r, n_ctx)).start()
    for k in range(1, CHUNKS):
        send_own(k)

    peers = [lax.rem(tp + r, n_tp) for r in range(1, n_tp)]
    if split:
        for q in peers:
            spread_copy(me, q, a_send.at[me]).start()

    grads = g_buf.at[me]

    def part_piece(i):
        load_w(i).wait()
        rows_all = grads[...].reshape(-1, g_buf.shape[3])
        piece = lax.dot_general(
            rows_all, w_buf[i], (((1,), (1,)), ((), ())), preferred_element_type=jnp.float32
        ).astype(jnp.bfloat16)
        part[:, :, i * d_tile : (i + 1) * d_tile] = piece.reshape(n_tp, rows, d_tile)

    per = -(-n_d // n_ctx)
    done = 0
    for r in range(1, n_ctx):
        for i in range(done, min(done + per, n_d)):
            part_piece(i)
        done = min(done + per, n_d)
        s = lax.rem(me - r + n_ctx, n_ctx)
        act_landing(s).wait_recv()
        if split:
            for q in peers:
                spread_copy(s, q).start()
    for i in range(done, n_d):
        part_piece(i)
    if not split:
        for q in peers:
            spread_all(q).start()

    def part_copy(q):
        return remote(part.at[q], landed.at[tp], p_ssem.at[q], p_rsem.at[tp], (me, q))

    def part_landing(q):
        return remote(part.at[q], landed.at[q], p_ssem.at[q], p_rsem.at[q], (me, q))

    for q in peers:
        part_copy(q).start()

    n_cols = g_buf.shape[3]
    n_tile = 512 if n_cols % 512 == 0 else n_cols

    def accumulate(zz, first, k=None):
        if k is None:
            lhs = a_buf[pl.ds(2 * zz, 2)].reshape(-1, feats).T
        else:
            size = n_tp // CHUNKS
            lhs = a_buf[pl.ds(2 * zz, 2), k * size : (k + 1) * size].reshape(-1, feats).T

        for j in range(n_cols // n_tile):
            cols = slice(j * n_tile, (j + 1) * n_tile)
            if k is None:
                rhs = g_buf[pl.ds(2 * zz, 2), :, :, cols].reshape(-1, n_tile)
            else:
                rhs = g_buf[pl.ds(2 * zz, 2), k, :, cols].reshape(-1, n_tile)
            term = jnp.dot(lhs, rhs, preferred_element_type=jnp.float32) * scale
            if first:
                gw_ref[:, cols] = term
            else:
                gw_ref[:, cols] += term

    def await_acts(zz, first):
        if split:
            for c in range(2):
                for q in peers:
                    spread_landing(2 * zz + c, q).wait_recv()
        elif first:
            for q in peers:
                spread_all_landing(q).wait_recv()

    def chip_terms(zz, first=False):
        other = 2 * zz + 1 - core
        for k in range(CHUNKS):
            across(other, k).wait_recv()
        await_acts(zz, first)
        accumulate(zz, first)

    def terms_at(d):
        if d == 0:
            chip_terms(z, True)
            return

        @pl.when(z >= d)
        def _():
            chip_terms(z - d)

        @pl.when(z + d < n_line)
        def _():
            chip_terms(z + d)

    def sum_parts():
        for q in peers:
            part_landing(q).wait_recv()
        total = part[tp].astype(jnp.float32)
        for q in peers:
            total = total + landed[q].astype(jnp.float32)
        gin_ref[...] = total.astype(jnp.bfloat16)

    def from_below(d, k):
        s = me - 2 * d
        up(s, k).wait_recv()

        @pl.when(has_up)
        def _():
            up(s, k).start()

        across(s, k).start()

    def from_above(d, k):
        s = me + 2 * d
        down(s, k).wait_recv()

        @pl.when(has_down)
        def _():
            down(s, k).start()

        across(s, k).start()

    for d in range(1, n_line - 1):
        for k in range(CHUNKS):

            @pl.when(z >= d)
            def _():
                from_below(d, k)

            @pl.when(z + d < n_line)
            def _():
                from_above(d, k)

        terms_at(d - 1)

    d = n_line - 1
    terms_at(d - 1)

    def last_terms(zz, arrive):
        other = 2 * zz + 1 - core
        await_acts(zz, False)
        for k in range(CHUNKS):
            arrive(d, k)
            if k == CHUNKS - 1:
                sum_parts()
            if k > 0:
                across(other, k - 1).wait_recv()
                accumulate(zz, False, k - 1)
        across(other, CHUNKS - 1).wait_recv()
        accumulate(zz, False, CHUNKS - 1)

    @pl.when(z == d)
    def _():
        last_terms(0, from_below)

    @pl.when(z == 0)
    def _():
        last_terms(d, from_above)

    @pl.when((z > 0) & (z < d))
    def _():
        sum_parts()

    for r in range(1, n_ctx):
        act_copy(lax.rem(me + r, n_ctx)).wait_send()
    for q in peers:
        part_copy(q).wait_send()
        if split:
            for s in range(n_ctx):
                spread_copy(s, q).wait_send()
        else:
            spread_all(q).wait_send()
    for zz in range(n_line):
        for k in range(CHUNKS):
            s = 2 * zz + core
            across(s, k).wait_send()

            @pl.when(has_up & (zz <= z))
            def _():
                up(s, k).wait_send()

            @pl.when(has_down & (zz >= z))
            def _():
                down(s, k).wait_send()


def body(act_codes, scale_exps, weight, grad_out):
    n_ctx, n_tp = lax.axis_size("ctx"), lax.axis_size("tp")
    n_line = n_ctx // 2
    rows, width = act_codes.shape
    toks, cols = grad_out.shape
    feats = width // n_ctx
    d_tile = min(512, width)
    dma = pltpu.SemaphoreType.DMA
    lanes = -(-cols // 128) * 128
    outs = -(-rows // 16) * 16 * width * 2 + feats * lanes * 4
    vmem = pl.BlockSpec(memory_space=pltpu.VMEM)
    hbm = pl.BlockSpec(memory_space=pltpu.HBM)
    bf16 = jnp.bfloat16
    return pl.pallas_call(
        functools.partial(kernel, n_ctx, n_tp, toks * n_ctx),
        out_shape=(
            pltpu.VMEM((rows, width), bf16),
            pltpu.VMEM((feats, cols), jnp.float32),
        ),
        in_specs=[hbm, hbm, hbm, hbm],
        out_specs=(vmem, vmem),
        scratch_shapes=[
            pltpu.VMEM((rows, width), bf16),
            pltpu.VMEM(scale_exps.shape[::-1], scale_exps.dtype),
            pltpu.VMEM((width // d_tile, d_tile, cols), bf16),
            pltpu.VMEM((n_ctx, CHUNKS, toks // CHUNKS, cols), bf16),
            pltpu.VMEM((n_ctx, rows, feats), bf16),
            pltpu.VMEM((n_ctx, n_tp, rows, feats), bf16),
            pltpu.VMEM((n_tp, rows, width), bf16),
            pltpu.VMEM((n_tp, rows, width), bf16),
            dma((2,)),
            dma((width // d_tile,)),
            dma((CHUNKS,)),
            dma((n_ctx,)),
            dma((n_ctx,)),
            dma((n_ctx if n_ctx * n_tp <= 64 else 1, n_tp)),
            dma((n_ctx if n_ctx * n_tp <= 64 else 1, n_tp)),
            dma((n_line, CHUNKS)),
            dma((n_line, CHUNKS)),
            dma((n_line, CHUNKS)),
            dma((n_ctx, CHUNKS)),
            dma((n_tp,)),
            dma((n_tp,)),
        ],
        compiler_params=pltpu.CompilerParams(
            collective_id=0, has_side_effects=True, vmem_limit_bytes=67_043_328 - outs - 8192
        ),
    )(act_codes, scale_exps.T, weight, grad_out)


def solution(mesh):
    placed = (P(("ctx", "tp"), None), P(("ctx", "tp"), None), P(None, "tp"), P("ctx", "tp"))
    return jax.shard_map(
        body,
        mesh=mesh,
        in_specs=placed,
        out_specs=(P(("ctx", "tp"), None), P("ctx", "tp")),
        check_vma=False,
    )
```

profile of v0, /device:TPU:0, one launch (start us, length us, event | category | flops | bytes accessed | tf_op | source)
XLA Modules:
  0.0 72.7 jit_solution(14699198809055646251)
XLA Ops:
  0.6 69.6 %shard_map.59 = (bf16[64,4096]{1,0:T(8,128)(2,1)S(1)}, f32[512,1536]{1,0:T(8,128)S(1)}) custom-call(bf16[64,4096]{1,0:T(8,128)(2,1)} %codes_hbm.1, s32[32,64]{1,0:T(8,128)} %bitcast.1, bf16[4096,1536]{1,0:T(8,128)(2,1)} %weight_ref.1, bf16[256,1536]{1,0:T(8,128)(2,1)} %grads_ref.1), custom_call_target="tpu_custom_call" | custom-call | tf_op jit(solution)/shard_map/pallas_call | solution.py:349
  70.2 0.8 %copy.8 = bf16[64,4096]{1,0:T(8,128)(2,1)} copy(bf16[64,4096]{1,0:T(8,128)(2,1)S(1)} %get-tuple-element.2) | data formatting | bytes 1048576
  71.0 1.7 %copy.9 = f32[512,1536]{1,0:T(8,128)} copy(f32[512,1536]{1,0:T(8,128)S(1)} %get-tuple-element.3) | data formatting | bytes 6291456
where the time goes:
time: 73 us; the launch traced here: 72.7 us
  Pallas kernels  69.6 us (95%)
  local copies, waits for them, and re-layouts  2.46 us (3%)
    pallas_call x1, Pallas kernels, body(): pl.pallas_call(functools.partial(kernel, n_ctx, n_tp, toks * n_ctx), out_...  69.6 us
    unnamed x2, local copies, waits for them, and re-layouts  2.46 us

commit v1 on v0

--- a/solution.py
+++ b/solution.py
@@ -11,7 +11,7 @@
 CHUNKS = 4
 
 
-def kernel(
+def line_kernel(
     n_ctx, n_tp, tokens,
     codes_hbm, exps_hbm, weight_ref, grads_ref,
     gin_ref, gw_ref,
@@ -333,7 +333,7 @@
                 down(s, k).wait_send()
 
 
-def body(act_codes, scale_exps, weight, grad_out):
+def line_body(act_codes, scale_exps, weight, grad_out):
     n_ctx, n_tp = lax.axis_size("ctx"), lax.axis_size("tp")
     n_line = n_ctx // 2
     rows, width = act_codes.shape
@@ -347,7 +347,7 @@
     hbm = pl.BlockSpec(memory_space=pltpu.HBM)
     bf16 = jnp.bfloat16
     return pl.pallas_call(
-        functools.partial(kernel, n_ctx, n_tp, toks * n_ctx),
+        functools.partial(line_kernel, n_ctx, n_tp, toks * n_ctx),
         out_shape=(
             pltpu.VMEM((rows, width), bf16),
             pltpu.VMEM((feats, cols), jnp.float32),
@@ -383,6 +383,480 @@
     )(act_codes, scale_exps.T, weight, grad_out)
 
 
+RAW = 1
+WIDE = 256
+
+
+def blocks_of(cols):
+    full = cols // WIDE - 1
+    return [(b * WIDE, WIDE) for b in range(full)] + [
+        (full * WIDE + i * (WIDE // 2), WIDE // 2) for i in range(2)
+    ]
+
+
+def square_kernel(
+    n_ctx, n_tp, tokens,
+    codes_hbm, exps_hbm, weight_ref, grads_ref,
+    gin_ref, gw_ref,
+    codes_ref, exps_ref, w_buf, g_own, g_wide, g_slim, a_send, a_buf, p_buf, a_t, p_t,
+    part, recv1, total1, recv2, sums_out, sums_in, slim_out, slim_in,
+    in_sem, w_sem, g_sem,
+    a_ssem, a_rsem, p_rsem, fwd_ssem, spread_ssem, g_ssem, g_rsem,
+    one_ssem, one_rsem, two_ssem, two_rsem, s_ssem, s_rsem,
+):
+    me = lax.axis_index("ctx")
+    tp = lax.axis_index("tp")
+    core = lax.rem(me, 2)
+    z = lax.div(me, 2)
+    mate = me + 1 - 2 * core
+    n_line = n_ctx // 2
+    side = lax.div(z, 2)
+    z_end, z_mid = (n_line - 1) * side, 1 + side
+    z_far_mid, z_far_end = 2 - side, (n_line - 1) * (1 - side)
+    y, x = lax.div(tp, 2), lax.rem(tp, 2)
+    by_x, by_y = 2 * y + 1 - x, 2 * (1 - y) + x
+    near = by_x + core * (by_y - by_x)
+    next_ = by_y + core * (by_x - by_y)
+    diag = n_tp - 1 - tp
+    rows, width = codes_ref.shape
+    toks = g_own.shape[0]
+    block = width // exps_ref.shape[0]
+    feats = width // n_ctx
+    d_tile = w_buf.shape[1]
+    n_d = w_buf.shape[0]
+    chip = 2 * toks
+    scale = lax.rsqrt(jnp.float32(tokens))
+    blocks = blocks_of(g_own.shape[1])
+    n_b = len(blocks)
+    full = n_b - 2
+
+    def g_at(b):
+        return g_wide.at[b] if b < full else g_slim.at[b - full]
+
+    def g_piece(s, b):
+        return g_at(b).at[pl.ds(s * toks, toks)]
+
+    def load_w(i):
+        return pltpu.make_async_copy(
+            weight_ref.at[pl.ds(i * d_tile, d_tile)], w_buf.at[i], w_sem.at[i]
+        )
+
+    def load_g(b):
+        start, size = blocks[b]
+        return pltpu.make_async_copy(
+            grads_ref.at[:, pl.ds(start, size)], g_piece(me, b), g_sem.at[b]
+        )
+
+    load_codes = pltpu.make_async_copy(codes_hbm, codes_ref, in_sem.at[0])
+    load_exps = pltpu.make_async_copy(exps_hbm, exps_ref, in_sem.at[1])
+    load_own = pltpu.make_async_copy(grads_ref, g_own, in_sem.at[2])
+    load_g(0).start()
+    load_codes.start()
+    load_exps.start()
+    load_g(1).start()
+    load_own.start()
+    load_w(0).start()
+    for b in range(2, n_b):
+        load_g(b).start()
+    for i in range(1, n_d):
+        load_w(i).start()
+
+    barrier = pltpu.get_barrier_semaphore()
+    for r in range(1, n_ctx):
+        pl.semaphore_signal(
+            barrier, inc=1, device_id=(lax.rem(me + r, n_ctx), tp), device_id_type=MESH
+        )
+    for r in range(1, n_tp):
+        pl.semaphore_signal(
+            barrier, inc=1, device_id=(me, lax.rem(tp + r, n_tp)), device_id_type=MESH
+        )
+    pl.semaphore_wait(barrier, n_ctx + n_tp - 2)
+
+    def dequantize():
+        load_codes.wait()
+        load_exps.wait()
+        powers = jnp.exp2(exps_ref[...].astype(jnp.float32)).T
+        for b in range(width // block):
+            owner, place = divmod(b * block, feats)
+            value = codes_ref[:, b * block : (b + 1) * block].astype(jnp.float32)
+            value = value * powers[:, b : b + 1]
+            a_send[owner, :, place : place + block] = value.astype(jnp.bfloat16)
+        a_buf[me, tp] = a_send[me]
+
+    def program(is_mid):
+        pending = []
+
+        def send(src, dst, ssem, rsem, to):
+            copy = pltpu.make_async_remote_copy(
+                src_ref=src, dst_ref=dst, send_sem=ssem, recv_sem=rsem,
+                device_id=to, device_id_type=MESH,
+            )
+            copy.start()
+            pending.append(copy)
+
+        def landed(dst, ssem, rsem):
+            pltpu.make_async_remote_copy(
+                src_ref=dst, dst_ref=dst, send_sem=ssem, recv_sem=rsem,
+                device_id=(me, tp), device_id_type=MESH,
+            ).wait_recv()
+
+        def both(zz):
+            return (2 * zz, 2 * zz + 1)
+
+        acts, ends = (a_buf, a_rsem, 0), (p_buf, p_rsem, 1)
+
+        def act_send(d, to, kind):
+            buf, rsem, _ = kind
+            send(a_send.at[d], buf.at[me, tp], a_ssem.at[d], rsem.at[me, tp], (to, tp))
+
+        def spread(kind, s):
+            buf, rsem, k = kind
+            for n, q in enumerate((near, next_)):
+                send(buf.at[s, tp], buf.at[s, tp], spread_ssem.at[k, s, n], rsem.at[s, tp], (me, q))
+
+        def pass_end(s):
+            send(
+                p_buf.at[s, tp], a_buf.at[s, tp], fwd_ssem.at[s], a_rsem.at[s, tp],
+                (2 * z_end + core, tp),
+            )
+
+        def arrive(kind, s):
+            buf, rsem, k = kind
+            landed(buf.at[s, tp], spread_ssem.at[k, s, 0], rsem.at[s, tp])
+            spread(kind, s)
+            if k == 1:
+                pass_end(s)
+
+        def relay(kind, s):
+            buf, rsem, k = kind
+            landed(buf.at[s, near], spread_ssem.at[k, s, 2], rsem.at[s, near])
+            send(
+                buf.at[s, near], buf.at[s, near], spread_ssem.at[k, s, 2], rsem.at[s, near],
+                (me, next_),
+            )
+
+        def gathered(kind, s):
+            buf, rsem, k = kind
+            for q in (next_, diag):
+                landed(buf.at[s, q], spread_ssem.at[k, s, 2], rsem.at[s, q])
+
+        def turn(kind, zz):
+            buf, _, k = kind
+            for s in both(zz):
+                gathered(kind, s)
+            value = buf[pl.ds(2 * zz, 2)].reshape(chip, feats).T
+            if k == 0:
+                a_t[:, pl.ds(pl.multiple_of(zz * chip, chip), chip)] = value
+            else:
+                p_t[:, pl.ds(pl.multiple_of((zz - 1 + side) * chip, chip), chip)] = value
+
+        def g_send(s, b, way, to):
+            send(
+                g_piece(s, b), g_piece(s, b), g_ssem.at[way, lax.div(s, 2), b], g_rsem.at[s, b],
+                (to, tp),
+            )
+
+        inward = 2 * (z_far_mid if is_mid else z_mid) + core
+        outward = 2 * z_end + core
+
+        def g_await(s, b):
+            landed(g_piece(s, b), g_ssem.at[0, 0, b], g_rsem.at[s, b])
+
+        def g_mine(b):
+            load_g(b).wait()
+            g_send(me, b, 0, inward)
+            if is_mid and b < RAW:
+                g_send(me, b, 1, outward)
+            g_send(me, b, 2, mate)
+
+        def g_take(zz, b, on):
+            s = 2 * zz + core
+            g_await(s, b)
+            if on is not None:
+                g_send(s, b, on, inward if on == 0 else outward)
+            g_send(s, b, 2, mate)
+
+        def g_mates(zs, b):
+            for zz in zs:
+                g_await(2 * zz + 1 - core, b)
+
+        def piece(i):
+            if i == 0:
+                load_own.wait()
+            load_w(i).wait()
+            value = lax.dot_general(
+                g_own[...], w_buf[i], (((1,), (1,)), ((), ())), preferred_element_type=jnp.float32
+            ).astype(jnp.bfloat16)
+            value = value.reshape(n_tp, rows, d_tile)
+            for q in range(n_tp):
+                dy, dx = lax.rem(y + q // 2, 2), lax.rem(x + q % 2, 2)
+                slot = 2 * dx + dy + core * (dy - dx)
+                part[i, slot] = value[q]
+
+        def part_one(i):
+            send(part.at[i, pl.ds(2, 2)], recv1.at[i], one_ssem.at[i], one_rsem.at[i], (me, near))
+
+        def part_two(i):
+            landed(recv1.at[i], one_ssem.at[i], one_rsem.at[i])
+            total = part[i, 1].astype(jnp.float32) + recv1[i, 1].astype(jnp.float32)
+            total1[i] = total.astype(jnp.bfloat16)
+            send(total1.at[i], recv2.at[i], two_ssem.at[i], two_rsem.at[i], (me, next_))
+
+        def part_sum(i):
+            landed(recv2.at[i], two_ssem.at[i], two_rsem.at[i])
+            total = part[i, 0].astype(jnp.float32) + recv1[i, 0].astype(jnp.float32)
+            total = total + recv2[i].astype(jnp.float32)
+            gin_ref[:, i * d_tile : (i + 1) * d_tile] = total.astype(jnp.bfloat16)
+
+        def dot(lhs, rhs):
+            return jnp.dot(lhs, rhs, preferred_element_type=jnp.float32)
+
+        def cols(b):
+            start, size = blocks[b]
+            return slice(start, start + size)
+
+        def whole_block(b):
+            gw_ref[:, cols(b)] = dot(a_t[...], g_at(b)[...]) * scale
+
+        def out_at(b):
+            return sums_out.at[b - RAW] if b < full else slim_out.at[b - full]
+
+        def in_at(b):
+            return sums_in.at[b - RAW] if b < full else slim_in.at[b - full]
+
+        def sum_block(b):
+            first = pl.multiple_of((1 - side) * chip, chip)
+            rhs = g_at(b)[pl.ds(first, (n_line - 1) * chip)]
+            out_at(b)[...] = dot(p_t[...], rhs).astype(jnp.bfloat16)
+            send(out_at(b), in_at(b), s_ssem.at[b], s_rsem.at[b], (outward, tp))
+
+        def own_block(b):
+            here = pl.ds(pl.multiple_of(z_end * chip, chip), chip)
+            gw_ref[:, cols(b)] = dot(a_t[:, here], g_at(b)[here])
+
+        def add_block(b):
+            landed(in_at(b), s_ssem.at[b], s_rsem.at[b])
+            gw_ref[:, cols(b)] = (gw_ref[:, cols(b)] + in_at(b)[...].astype(jnp.float32)) * scale
+
+        others = (z_mid, z_far_mid, z_far_end)
+        g_mine(0)
+        dequantize()
+        if is_mid:
+            p_buf[me, tp] = a_send[2 * z_end + core]
+            for c in range(2):
+                act_send(2 * z_far_end + c, 2 * z_far_mid + c, ends)
+            pass_end(me)
+            act_send(2 * z_end + 1 - core, mate, ends)
+            spread(ends, me)
+            g_mine(1)
+            for c in range(2):
+                act_send(2 * z_far_mid + c, 2 * z_far_mid + c, acts)
+            act_send(mate, mate, acts)
+            spread(acts, me)
+            piece(0)
+            arrive(ends, mate)
+            arrive(acts, mate)
+            piece(1)
+            relay(ends, me)
+            relay(ends, mate)
+            piece(2)
+            relay(acts, me)
+            relay(acts, mate)
+            piece(3)
+            for s in both(z_far_mid):
+                arrive(ends, s)
+            piece(4)
+            g_take(z_end, 0, 0)
+            for s in both(z_far_end):
+                arrive(ends, s)
+            piece(5)
+            for s in both(z_far_mid):
+                relay(ends, s)
+            piece(6)
+            piece(7)
+            for s in both(z_far_end):
+                relay(ends, s)
+            g_take(z_far_mid, 0, 1)
+            g_take(z_end, 1, 0)
+            g_mine(2)
+            for i in range(4):
+                part_one(i)
+            for zz in (z_end, z_far_mid, z_far_end):
+                for s in both(zz):
+                    arrive(acts, s)
+            for i in range(4, n_d):
+                part_one(i)
+            for zz in (z_end, z_far_mid, z_far_end):
+                for s in both(zz):
+                    relay(acts, s)
+            for zz in others:
+                turn(ends, zz)
+            g_take(z_far_end, 0, 1)
+            for zz in (z_mid, z_end, z_far_mid, z_far_end):
+                turn(acts, zz)
+            for b in range(n_b):
+                if b > 0:
+                    if b + 1 < n_b:
+                        g_take(z_end, b + 1, 0)
+                    if b + 2 < n_b:
+                        g_mine(b + 2)
+                    g_take(z_far_mid, b, 1 if b < RAW else None)
+                    g_take(z_far_end, b, 1 if b < RAW else None)
+                g_mates((z_mid, z_end, z_far_mid, z_far_end), b)
+                if b >= RAW:
+                    sum_block(b)
+                whole_block(b)
+                if 0 < b < 5:
+                    part_two(2 * b - 2)
+                    part_two(2 * b - 1)
+                if b == 5:
+                    for i in range(n_d):
+                        part_sum(i)
+        else:
+            for c in range(2):
+                act_send(2 * z_far_end + c, 2 * z_far_mid + c, ends)
+            g_mine(1)
+            spread(acts, me)
+            act_send(mate, mate, acts)
+            for c in range(2):
+                act_send(2 * z_far_mid + c, 2 * z_far_mid + c, acts)
+            for c in range(2):
+                act_send(2 * z_mid + c, 2 * z_mid + c, acts)
+            for b in range(2, n_b):
+                g_mine(b)
+            piece(0)
+            arrive(acts, mate)
+            piece(1)
+            relay(acts, me)
+            relay(acts, mate)
+            piece(2)
+            for s in both(z_mid):
+                arrive(acts, s)
+            piece(3)
+            piece(4)
+            for s in both(z_mid):
+                relay(acts, s)
+            g_take(z_mid, 0, None)
+            piece(5)
+            for s in both(z_far_mid):
+                arrive(acts, s)
+            piece(6)
+            piece(7)
+            for i in range(4):
+                part_one(i)
+            for s in both(z_far_end):
+                arrive(acts, s)
+            for i in range(4, n_d):
+                part_one(i)
+            for zz in (z_far_mid, z_far_end):
+                for s in both(zz):
+                    relay(acts, s)
+            turn(acts, z_end)
+            for b in range(RAW, n_b):
+                g_mates((z_end,), b)
+                own_block(b)
+            g_take(z_far_mid, 0, None)
+            for i in range(n_d // 2):
+                part_two(i)
+            for zz in others:
+                turn(acts, zz)
+            g_take(z_far_end, 0, None)
+            g_mates((z_end,) + others, 0)
+            whole_block(0)
+            for i in range(n_d // 2, n_d):
+                part_two(i)
+            for b in range(RAW, n_b):
+                add_block(b)
+                if b == n_b - 3:
+                    for i in range(n_d):
+                        part_sum(i)
+        for copy in pending:
+            copy.wait_send()
+
+    is_mid = (z == z_mid)
+
+    @pl.when(is_mid)
+    def _():
+        program(True)
+
+    @pl.when(jnp.logical_not(is_mid))
+    def _():
+        program(False)
+
+
+def square_body(act_codes, scale_exps, weight, grad_out):
+    n_ctx, n_tp = lax.axis_size("ctx"), lax.axis_size("tp")
+    rows, width = act_codes.shape
+    toks, cols = grad_out.shape
+    feats = width // n_ctx
+    d_tile = width // 8
+    n_d = width // d_tile
+    all_toks = toks * n_ctx
+    n_b = len(blocks_of(cols))
+    full = n_b - 2
+    dma = pltpu.SemaphoreType.DMA
+    vmem = pl.BlockSpec(memory_space=pltpu.VMEM)
+    hbm = pl.BlockSpec(memory_space=pltpu.HBM)
+    bf16 = jnp.bfloat16
+    outs = rows * width * 2 + feats * cols * 4
+    return pl.pallas_call(
+        functools.partial(square_kernel, n_ctx, n_tp, all_toks),
+        out_shape=(
+            pltpu.VMEM((rows, width), bf16),
+            pltpu.VMEM((feats, cols), jnp.float32),
+        ),
+        in_specs=[hbm, hbm, hbm, hbm],
+        out_specs=(vmem, vmem),
+        scratch_shapes=[
+            pltpu.VMEM((rows, width), bf16),
+            pltpu.VMEM(scale_exps.shape[::-1], scale_exps.dtype),
+            pltpu.VMEM((n_d, d_tile, cols), bf16),
+            pltpu.VMEM((toks, cols), bf16),
+            pltpu.VMEM((full, all_toks, WIDE), bf16),
+            pltpu.VMEM((2, all_toks, WIDE // 2), bf16),
+            pltpu.VMEM((n_ctx, rows, feats), bf16),
+            pltpu.VMEM((n_ctx, n_tp, rows, feats), bf16),
+            pltpu.VMEM((n_ctx, n_tp, rows, feats), bf16),
+            pltpu.VMEM((feats, all_toks), bf16),
+            pltpu.VMEM((feats, all_toks - 2 * toks), bf16),
+            pltpu.VMEM((n_d, n_tp, rows, d_tile), bf16),
+            pltpu.VMEM((n_d, 2, rows, d_tile), bf16),
+            pltpu.VMEM((n_d, rows, d_tile), bf16),
+            pltpu.VMEM((n_d, rows, d_tile), bf16),
+            pltpu.VMEM((full - RAW, feats, WIDE), bf16),
+            pltpu.VMEM((full - RAW, feats, WIDE), bf16),
+            pltpu.VMEM((2, feats, WIDE // 2), bf16),
+            pltpu.VMEM((2, feats, WIDE // 2), bf16),
+            dma((3,)),
+            dma((n_d,)),
+            dma((n_b,)),
+            dma((n_ctx,)),
+            dma((n_ctx, n_tp)),
+            dma((n_ctx, n_tp)),
+            dma((n_ctx,)),
+            dma((2, n_ctx, 3)),
+            dma((3, n_ctx // 2, n_b)),
+            dma((n_ctx, n_b)),
+            dma((n_d,)),
+            dma((n_d,)),
+            dma((n_d,)),
+            dma((n_d,)),
+            dma((n_b,)),
+            dma((n_b,)),
+        ],
+        compiler_params=pltpu.CompilerParams(
+            collective_id=0, has_side_effects=True, vmem_limit_bytes=67_043_328 - outs - 8192
+        ),
+    )(act_codes, scale_exps.T, weight, grad_out)
+
+
+def body(act_codes, scale_exps, weight, grad_out):
+    line, square = lax.axis_size("ctx") // 2, lax.axis_size("tp")
+    if line == 4 and square == 4 and grad_out.shape[1] % WIDE == 0:
+        return square_body(act_codes, scale_exps, weight, grad_out)
+    return line_body(act_codes, scale_exps, weight, grad_out)
+
+
 def solution(mesh):
     placed = (P(("ctx", "tp"), None), P(("ctx", "tp"), None), P(None, "tp"), P("ctx", "tp"))
     return jax.shard_map(

time: 73 us -> 87.9 us (1.20)
  Pallas kernels: 69.6 us -> 84.7 us
    pallas_call x1, Pallas kernels: 69.6 us -> 84.7 us  [square_body(): pl.pallas_call(functools.partial(square_kernel, n_ctx, n_tp, all_toks), o...]
where the time goes in v1:
time: 87.9 us; the launch traced here: 87.8 us
  Pallas kernels  84.7 us (96%)
  local copies, waits for them, and re-layouts  2.46 us (3%)
    pallas_call x1, Pallas kernels, square_body(): pl.pallas_call(functools.partial(square_kernel, n_ctx, n_tp, all_toks), o...  84.7 us
    unnamed x2, local copies, waits for them, and re-layouts  2.46 us

profile of v1, /device:TPU:0, one launch (start us, length us, event | category | flops | bytes accessed | tf_op | source)
XLA Modules:
  0.0 87.8 jit_solution(409920660723702465)
XLA Ops:
  0.6 84.7 %shard_map.59 = (bf16[64,4096]{1,0:T(8,128)(2,1)S(1)}, f32[512,1536]{1,0:T(8,128)S(1)}) custom-call(bf16[64,4096]{1,0:T(8,128)(2,1)} %codes_hbm.1, s32[32,64]{1,0:T(8,128)} %bitcast.1, bf16[4096,1536]{1,0:T(8,128)(2,1)} %weight_ref.1, bf16[256,1536]{1,0:T(8,128)(2,1)} %grads_ref.1), custom_call_target="tpu_custom_call" | custom-call | tf_op jit(solution)/shard_map/pallas_call | solution.py:802
  85.3 0.8 copy.8
  86.1 1.7 %copy.9 = f32[512,1536]{1,0:T(8,128)} copy(f32[512,1536]{1,0:T(8,128)S(1)} %get-tuple-element.3) | data formatting | bytes 6291456

commit v2 on v0

--- a/solution.py
+++ b/solution.py
@@ -1,4 +1,5 @@
 import functools
+import math
 
 import jax
 import jax.numpy as jnp
@@ -11,7 +12,7 @@
 CHUNKS = 4
 
 
-def kernel(
+def line_kernel(
     n_ctx, n_tp, tokens,
     codes_hbm, exps_hbm, weight_ref, grads_ref,
     gin_ref, gw_ref,
@@ -333,7 +334,7 @@
                 down(s, k).wait_send()
 
 
-def body(act_codes, scale_exps, weight, grad_out):
+def line_body(act_codes, scale_exps, weight, grad_out):
     n_ctx, n_tp = lax.axis_size("ctx"), lax.axis_size("tp")
     n_line = n_ctx // 2
     rows, width = act_codes.shape
@@ -347,7 +348,7 @@
     hbm = pl.BlockSpec(memory_space=pltpu.HBM)
     bf16 = jnp.bfloat16
     return pl.pallas_call(
-        functools.partial(kernel, n_ctx, n_tp, toks * n_ctx),
+        functools.partial(line_kernel, n_ctx, n_tp, toks * n_ctx),
         out_shape=(
             pltpu.VMEM((rows, width), bf16),
             pltpu.VMEM((feats, cols), jnp.float32),
@@ -383,6 +384,613 @@
     )(act_codes, scale_exps.T, weight, grad_out)
 
 
+RAW = 2
+WIDE = 256
+
+
+def wide_blocks(cols):
+    return cols // WIDE * 3 // 6
+
+
+def blocks_of(cols):
+    full = wide_blocks(cols)
+    slim = WIDE // 2
+    return [(b * WIDE, WIDE) for b in range(full)] + [
+        (start, slim) for start in range(full * WIDE, cols, slim)
+    ]
+
+
+def square_kernel(
+    n_ctx, n_tp, tokens,
+    codes_hbm, exps_hbm, weight_ref, grads_ref,
+    gin_ref, gw_ref,
+    codes_ref, exps_ref, w_buf, g_own, g_wide, g_slim, a_send, a_buf, p_buf, a_t, p_t,
+    part, recv1, total1, recv2, sums_out, sums_in, slim_out, slim_in,
+    in_sem, w_sem, g_sem, s_sem, line_sem, near_sem, rest_sem, g_rsem, mate_sem,
+    one_sem, two_sem, sum_sem,
+):
+    me = lax.axis_index("ctx")
+    tp = lax.axis_index("tp")
+    core = lax.rem(me, 2)
+    z = lax.div(me, 2)
+    mate = me + 1 - 2 * core
+    n_line = n_ctx // 2
+    side = lax.div(z, 2)
+    z_end, z_mid = (n_line - 1) * side, 1 + side
+    z_far_mid, z_far_end = 2 - side, (n_line - 1) * (1 - side)
+    y, x = lax.div(tp, 2), lax.rem(tp, 2)
+    by_x, by_y = 2 * y + 1 - x, 2 * (1 - y) + x
+    near = by_x + core * (by_y - by_x)
+    next_ = by_y + core * (by_x - by_y)
+    diag = n_tp - 1 - tp
+    rows, width = codes_ref.shape
+    toks = g_own.shape[0]
+    block = width // exps_ref.shape[0]
+    feats = width // n_ctx
+    d_tile = w_buf.shape[1]
+    n_d = w_buf.shape[0]
+    chip = 2 * toks
+    unit = rows * feats
+    scale = lax.rsqrt(jnp.float32(tokens))
+    blocks = blocks_of(g_own.shape[1])
+    n_b = len(blocks)
+    full = g_wide.shape[0]
+
+    def g_at(b):
+        return g_wide.at[b] if b < full else g_slim.at[b - full]
+
+    def g_piece(s, b):
+        return g_at(b).at[pl.ds(s * toks, toks)]
+
+    def load_w(i):
+        return pltpu.make_async_copy(
+            weight_ref.at[pl.ds(i * d_tile, d_tile)], w_buf.at[i], w_sem.at[i % 2]
+        )
+
+    def load_g(b):
+        start, size = blocks[b]
+        return pltpu.make_async_copy(
+            grads_ref.at[:, pl.ds(start, size)], g_piece(me, b), g_sem.at[b]
+        )
+
+    load_codes = pltpu.make_async_copy(codes_hbm, codes_ref, in_sem.at[0])
+    load_exps = pltpu.make_async_copy(exps_hbm, exps_ref, in_sem.at[1])
+    load_own = pltpu.make_async_copy(grads_ref, g_own, in_sem.at[2])
+    load_codes.start()
+    load_exps.start()
+    load_g(0).start()
+    load_g(1).start()
+
+    barrier = pltpu.get_barrier_semaphore()
+    for r in range(1, n_ctx):
+        pl.semaphore_signal(
+            barrier, inc=1, device_id=(lax.rem(me + r, n_ctx), tp), device_id_type=MESH
+        )
+    for r in range(1, n_tp):
+        pl.semaphore_signal(
+            barrier, inc=1, device_id=(me, lax.rem(tp + r, n_tp)), device_id_type=MESH
+        )
+    load_exps.wait()
+    load_codes.wait()
+    load_own.start()
+    load_w(0).start()
+    for b in range(2, n_b):
+        load_g(b).start()
+    load_w(1).start()
+    powers = jnp.exp2(exps_ref[...].astype(jnp.float32)).T
+    for b in range(width // block):
+        owner, place = divmod(b * block, feats)
+        value = codes_ref[:, b * block : (b + 1) * block].astype(jnp.float32)
+        value = value * powers[:, b : b + 1]
+        a_send[owner, :, place : place + block] = value.astype(jnp.bfloat16)
+    a_buf[me, tp] = a_send[me]
+    p_buf[me, tp] = a_send[2 * (z_mid + z_end - z) + core]
+    pl.semaphore_wait(barrier, n_ctx + n_tp - 2)
+
+    def program(is_mid):
+        sent = {}
+
+        def remote(src, dst, ssem, rsem, to):
+            return pltpu.make_async_remote_copy(
+                src_ref=src, dst_ref=dst, send_sem=ssem, recv_sem=rsem,
+                device_id=to, device_id_type=MESH,
+            )
+
+        def send(kind, src, dst, rsem, to):
+            remote(src, dst, s_sem.at[kind], rsem, to).start()
+            sent[kind] = sent.get(kind, 0) + math.prod(src.shape) // unit
+
+        def landed(dst, rsem):
+            remote(dst, dst, s_sem.at[0], rsem, (me, tp)).wait_recv()
+
+        def all_sent():
+            for kind, n in sent.items():
+                if n % 24 == 0:
+                    ref = w_buf.at[pl.ds(0, n // 24)]
+                elif n % 2 == 0 and n // 2 <= n_d:
+                    ref = recv1.at[pl.ds(0, n // 2)]
+                elif n <= n_d:
+                    ref = recv2.at[pl.ds(0, n)]
+                else:
+                    ref = a_buf.at[pl.ds(0, n // n_tp)]
+                assert math.prod(ref.shape) == n * unit
+                remote(ref, ref, s_sem.at[kind], near_sem.at[0, 0], (me, tp)).wait_send()
+
+        def both(zz):
+            return (2 * zz, 2 * zz + 1)
+
+        acts, ends = (a_buf, 0), (p_buf, 1)
+
+        def act_send(d, to, kind):
+            buf, k = kind
+            send(0, a_send.at[d], buf.at[me, tp], line_sem.at[k, me], (to, tp))
+
+        def spread(kind, s):
+            buf, k = kind
+            send(1, buf.at[s, tp], buf.at[s, tp], near_sem.at[k, s], (me, near))
+            send(2, buf.at[s, tp], buf.at[s, tp], rest_sem.at[k, lax.div(s, 2)], (me, next_))
+
+        def pass_end(s):
+            send(3, p_buf.at[s, tp], a_buf.at[s, tp], line_sem.at[0, s], (2 * z_end + core, tp))
+
+        def arrive(kind, s):
+            buf, k = kind
+            landed(buf.at[s, tp], line_sem.at[k, s])
+            spread(kind, s)
+            if k == 1 and is_mid:
+                pass_end(s)
+
+        def relay(kind, s):
+            buf, k = kind
+            landed(buf.at[s, near], near_sem.at[k, s])
+            send(4, buf.at[s, near], buf.at[s, near], rest_sem.at[k, lax.div(s, 2)], (me, next_))
+
+        def gathered(kind, zz):
+            buf, k = kind
+            landed(buf.at[2 * zz], rest_sem.at[k, zz])
+
+        def pass_back(s, q):
+            send(
+                3, p_buf.at[s, q], a_buf.at[s, q], rest_sem.at[0, lax.div(s, 2)],
+                (2 * z_mid + core, tp),
+            )
+
+        def turned(kind, zz):
+            buf, k = kind
+            value = buf[pl.ds(2 * zz, 2)].reshape(chip, feats).T
+            if k == 0:
+                a_t[:, pl.ds(pl.multiple_of(zz * chip, chip), chip)] = value
+            else:
+                p_t[:, pl.ds(pl.multiple_of((zz - 1 + side) * chip, chip), chip)] = value
+
+        def turn(kind, zz):
+            gathered(kind, zz)
+            turned(kind, zz)
+
+        def turn_whole(zz):
+            landed(a_buf.at[pl.ds(2 * zz, 2)], rest_sem.at[0, zz])
+            turned(acts, zz)
+
+        def g_send(kind, s, b, rsem, to):
+            send(kind, g_piece(s, b), g_piece(s, b), rsem, (to, tp))
+
+        inward = 2 * (z_far_mid if is_mid else z_mid) + core
+        outward = 2 * z_end + core
+        FROM_SIDE, FROM_MID, FROM_END = 0, 1, 2
+
+        def g_mine(b):
+            load_g(b).wait()
+            g_send(5, me, b, g_rsem.at[FROM_MID if is_mid else FROM_SIDE, b], inward)
+            if is_mid and b < RAW:
+                g_send(6, me, b, g_rsem.at[FROM_SIDE, b], outward)
+            g_send(7, me, b, mate_sem.at[b], mate)
+
+        def g_take(zz, way, b):
+            s = 2 * zz + core
+            landed(g_piece(s, b), g_rsem.at[way, b])
+            if is_mid and way == FROM_SIDE:
+                g_send(5, s, b, g_rsem.at[FROM_END, b], inward)
+            elif is_mid and b < RAW:
+                g_send(6, s, b, g_rsem.at[way, b], outward)
+            g_send(7, s, b, mate_sem.at[b], mate)
+
+        def g_mates(n, b):
+            landed(g_at(b).at[pl.ds(0, n * toks)], mate_sem.at[b])
+
+        def piece(i):
+            if i == 0:
+                load_own.wait()
+            load_w(i).wait()
+            if i + 2 < n_d:
+                load_w(i + 2).start()
+            value = lax.dot_general(
+                g_own[...], w_buf[i], (((1,), (1,)), ((), ())), preferred_element_type=jnp.float32
+            ).astype(jnp.bfloat16)
+            value = value.reshape(n_tp, rows, d_tile)
+            for q in range(n_tp):
+                dy, dx = lax.rem(y + q // 2, 2), lax.rem(x + q % 2, 2)
+                slot = 2 * dx + dy + core * (dy - dx)
+                part[i, slot] = value[q]
+
+        def part_one(i):
+            send(8, part.at[i, pl.ds(2, 2)], recv1.at[i], one_sem.at[i], (me, near))
+
+        def part_two(i):
+            landed(recv1.at[i], one_sem.at[i])
+            total = part[i, 1].astype(jnp.float32) + recv1[i, 1].astype(jnp.float32)
+            total1[i] = total.astype(jnp.bfloat16)
+            send(9, total1.at[i], recv2.at[i], two_sem.at[i], (me, next_))
+
+        def part_sum(i):
+            landed(recv2.at[i], two_sem.at[i])
+            total = part[i, 0].astype(jnp.float32) + recv1[i, 0].astype(jnp.float32)
+            total = total + recv2[i].astype(jnp.float32)
+            gin_ref[:, i * d_tile : (i + 1) * d_tile] = total.astype(jnp.bfloat16)
+
+        def dot(lhs, rhs):
+            return jnp.dot(lhs, rhs, preferred_element_type=jnp.float32)
+
+        halves = [slice(h * (feats // 2), (h + 1) * (feats // 2)) for h in range(2)]
+
+        def cols(b):
+            start, size = blocks[b]
+            return slice(start, start + size)
+
+        def whole_block(b):
+            for half in halves:
+                gw_ref[half, cols(b)] = dot(a_t[half], g_at(b)[...]) * scale
+
+        def whole_pair(b):
+            start, size = blocks[b]
+            for half in halves:
+                rhs = jnp.concatenate([g_at(b)[...], g_at(b + 1)[...]], axis=1)
+                gw_ref[half, start : start + 2 * size] = dot(a_t[half], rhs) * scale
+
+        def out_at(b):
+            return sums_out.at[b - RAW] if b < full else slim_out.at[b - full]
+
+        def in_at(b):
+            return sums_in.at[b - RAW] if b < full else slim_in.at[b - full]
+
+        def sum_block(b):
+            first = pl.multiple_of((1 - side) * chip, chip)
+            for half in halves:
+                rhs = g_at(b)[pl.ds(first, (n_line - 1) * chip)]
+                out_at(b)[half] = dot(p_t[half], rhs).astype(jnp.bfloat16)
+                send(10, out_at(b).at[half], in_at(b).at[half], sum_sem.at[b], (outward, tp))
+
+        def own_block(b):
+            here = pl.ds(pl.multiple_of(z_end * chip, chip), chip)
+            for half in halves:
+                gw_ref[half, cols(b)] = dot(a_t[half, here], g_at(b)[here])
+
+        def add_block(b):
+            landed(in_at(b), sum_sem.at[b])
+            gw_ref[:, cols(b)] = (gw_ref[:, cols(b)] + in_at(b)[...].astype(jnp.float32)) * scale
+
+        if is_mid:
+            g_mine(7)
+            g_mine(3)
+            for c in range(2):
+                act_send(2 * z_far_end + c, 2 * z_far_mid + c, ends)
+            g_mine(1)
+            pass_end(me)
+            act_send(2 * z_end + 1 - core, mate, ends)
+            spread(ends, me)
+            act_send(mate, mate, acts)
+            spread(acts, me)
+            piece(0)
+            piece(1)
+            arrive(acts, mate)
+            arrive(ends, mate)
+            piece(2)
+            piece(3)
+            piece(4)
+            piece(5)
+            g_take(z_far_mid, FROM_MID, 7)
+            relay(ends, me)
+            piece(6)
+            piece(7)
+            g_take(z_far_mid, FROM_MID, 3)
+            relay(acts, me)
+            arrive(ends, 2 * z_far_mid + core)
+            relay(acts, mate)
+            arrive(ends, 2 * z_far_mid + 1 - core)
+            relay(ends, mate)
+            g_take(z_end, FROM_SIDE, 0)
+            g_mine(0)
+            g_take(z_end, FROM_SIDE, 2)
+            g_mine(2)
+            relay(ends, 2 * z_far_mid + core)
+            g_take(z_far_mid, FROM_MID, 1)
+            relay(ends, 2 * z_far_mid + 1 - core)
+            turn(acts, z_mid)
+            part_one(0)
+            arrive(ends, 2 * z_far_end + core)
+            turn(ends, z_mid)
+            turn(ends, z_far_mid)
+            arrive(ends, 2 * z_far_end + 1 - core)
+            g_take(z_far_end, FROM_END, 0)
+            part_two(0)
+            relay(ends, 2 * z_far_end + core)
+            part_one(1)
+            part_one(2)
+            g_take(z_far_mid, FROM_MID, 0)
+            part_one(3)
+            g_take(z_end, FROM_SIDE, 3)
+            g_mine(4)
+            g_mine(5)
+            relay(ends, 2 * z_far_end + 1 - core)
+            part_one(4)
+            g_mates(n_line, 0)
+            g_take(z_end, FROM_SIDE, 5)
+            g_take(z_end, FROM_SIDE, 4)
+            part_sum(0)
+            part_one(5)
+            g_take(z_far_end, FROM_END, 2)
+            part_one(6)
+            part_two(1)
+            turn(ends, z_far_end)
+            g_take(z_far_mid, FROM_MID, 2)
+            g_take(z_end, FROM_SIDE, 6)
+            g_mine(6)
+            for c in range(2):
+                act_send(2 * z_far_mid + c, 2 * z_far_mid + c, acts)
+            part_two(2)
+            g_mates(n_line, 2)
+            sum_block(2)
+            g_take(z_far_end, FROM_END, 3)
+            part_two(3)
+            part_sum(1)
+            g_take(z_far_mid, FROM_MID, 4)
+            g_mates(n_line, 3)
+            sum_block(3)
+            g_take(z_far_mid, FROM_MID, 5)
+            part_sum(2)
+            part_two(4)
+            g_take(z_far_end, FROM_END, 5)
+            g_take(z_end, FROM_SIDE, 7)
+            g_take(z_end, FROM_SIDE, 1)
+            g_take(z_end, FROM_SIDE, 8)
+            g_mine(8)
+            part_one(7)
+            part_sum(3)
+            part_two(5)
+            g_mates(n_line, 5)
+            g_take(z_far_end, FROM_END, 4)
+            g_mates(n_line, 4)
+            sum_block(4)
+            part_two(6)
+            part_sum(4)
+            sum_block(5)
+            g_take(z_far_end, FROM_END, 6)
+            part_sum(5)
+            part_two(7)
+            g_take(z_far_mid, FROM_MID, 6)
+            arrive(acts, 2 * z_far_end + core)
+            part_sum(6)
+            g_mates(n_line, 6)
+            sum_block(6)
+            arrive(acts, 2 * z_far_mid + core)
+            part_sum(7)
+            arrive(acts, 2 * z_far_end + 1 - core)
+            arrive(acts, 2 * z_far_mid + 1 - core)
+            turn_whole(z_end)
+            relay(acts, 2 * z_far_end + core)
+            g_take(z_far_end, FROM_END, 7)
+            relay(acts, 2 * z_far_mid + core)
+            g_mates(n_line, 7)
+            sum_block(7)
+            relay(acts, 2 * z_far_end + 1 - core)
+            g_take(z_far_end, FROM_END, 1)
+            relay(acts, 2 * z_far_mid + 1 - core)
+            g_mates(n_line, 1)
+            g_take(z_far_end, FROM_END, 8)
+            g_take(z_far_mid, FROM_MID, 8)
+            turn(acts, z_far_end)
+            g_mates(n_line, 8)
+            sum_block(8)
+            turn(acts, z_far_mid)
+            whole_block(0)
+            whole_block(1)
+            whole_block(2)
+            whole_pair(3)
+            whole_pair(5)
+            whole_pair(7)
+        else:
+            act_send(2 * z_mid + 1 - core, mate, ends)
+            spread(ends, me)
+            act_send(mate, mate, acts)
+            g_mine(4)
+            g_mine(2)
+            g_mine(0)
+            pass_back(me, tp)
+            for c in range(2):
+                act_send(2 * z_far_end + c, 2 * z_far_mid + c, ends)
+            spread(acts, me)
+            piece(0)
+            arrive(ends, mate)
+            arrive(acts, mate)
+            piece(1)
+            part_one(0)
+            piece(2)
+            piece(3)
+            piece(4)
+            piece(5)
+            relay(ends, me)
+            piece(6)
+            piece(7)
+            relay(acts, me)
+            g_take(z_mid, FROM_SIDE, 1)
+            relay(ends, mate)
+            arrive(acts, 2 * z_mid + core)
+            part_one(1)
+            relay(acts, mate)
+            arrive(acts, 2 * z_mid + 1 - core)
+            part_one(2)
+            arrive(acts, 2 * z_far_mid + core)
+            part_two(0)
+            arrive(acts, 2 * z_far_mid + 1 - core)
+            gathered(ends, z_end)
+            pass_back(mate, next_)
+            pass_back(mate, tp)
+            g_mine(3)
+            g_mine(5)
+            g_mine(8)
+            pass_back(me, next_)
+            g_mine(6)
+            g_mine(1)
+            pass_back(me, diag)
+            g_mine(7)
+            pass_back(mate, near)
+            pass_back(mate, diag)
+            for c in range(2):
+                act_send(2 * z_far_mid + c, 2 * z_far_mid + c, acts)
+            pass_back(me, near)
+            relay(acts, 2 * z_mid + core)
+            part_one(3)
+            g_take(z_mid, FROM_SIDE, 0)
+            part_two(1)
+            turn(acts, z_end)
+            g_mates(1, 2)
+            own_block(2)
+            g_mates(1, 3)
+            own_block(3)
+            g_mates(1, 4)
+            own_block(4)
+            g_mates(1, 5)
+            own_block(5)
+            g_mates(1, 6)
+            own_block(6)
+            relay(acts, 2 * z_mid + 1 - core)
+            g_mates(1, 7)
+            own_block(7)
+            g_mates(1, 8)
+            own_block(8)
+            g_take(z_far_mid, FROM_MID, 1)
+            arrive(acts, 2 * z_far_end + core)
+            part_two(2)
+            part_sum(0)
+            arrive(acts, 2 * z_far_end + 1 - core)
+            relay(acts, 2 * z_far_mid + core)
+            relay(acts, 2 * z_far_mid + 1 - core)
+            part_one(4)
+            part_one(5)
+            part_one(6)
+            g_take(z_far_end, FROM_END, 0)
+            part_sum(1)
+            part_one(7)
+            part_two(3)
+            turn(acts, z_mid)
+            g_take(z_far_mid, FROM_MID, 0)
+            relay(acts, 2 * z_far_end + core)
+            g_mates(n_line, 0)
+            relay(acts, 2 * z_far_end + 1 - core)
+            part_sum(2)
+            part_two(4)
+            turn(acts, z_far_mid)
+            part_two(5)
+            part_sum(3)
+            add_block(2)
+            part_two(6)
+            turn(acts, z_far_end)
+            whole_block(0)
+            part_sum(4)
+            add_block(3)
+            part_two(7)
+            part_sum(5)
+            part_sum(6)
+            add_block(4)
+            part_sum(7)
+            add_block(5)
+            add_block(6)
+            add_block(7)
+            g_take(z_far_end, FROM_END, 1)
+            g_mates(n_line, 1)
+            whole_block(1)
+            add_block(8)
+        all_sent()
+
+    is_mid = z == z_mid
+
+    @pl.when(is_mid)
+    def _():
+        program(True)
+
+    @pl.when(jnp.logical_not(is_mid))
+    def _():
+        program(False)
+
+
+def square_body(act_codes, scale_exps, weight, grad_out):
+    n_ctx, n_tp = lax.axis_size("ctx"), lax.axis_size("tp")
+    rows, width = act_codes.shape
+    toks, cols = grad_out.shape
+    feats = width // n_ctx
+    d_tile = width // 8
+    n_d = width // d_tile
+    all_toks = toks * n_ctx
+    n_b = len(blocks_of(cols))
+    full = wide_blocks(cols)
+    dma = pltpu.SemaphoreType.DMA
+    vmem = pl.BlockSpec(memory_space=pltpu.VMEM)
+    hbm = pl.BlockSpec(memory_space=pltpu.HBM)
+    bf16 = jnp.bfloat16
+    outs = rows * width * 2 + feats * cols * 4
+    return pl.pallas_call(
+        functools.partial(square_kernel, n_ctx, n_tp, all_toks),
+        out_shape=(
+            pltpu.VMEM((rows, width), bf16),
+            pltpu.VMEM((feats, cols), jnp.float32),
+        ),
+        in_specs=[hbm, hbm, hbm, hbm],
+        out_specs=(vmem, vmem),
+        scratch_shapes=[
+            pltpu.VMEM((rows, width), bf16),
+            pltpu.VMEM(scale_exps.shape[::-1], scale_exps.dtype),
+            pltpu.VMEM((n_d, d_tile, cols), bf16),
+            pltpu.VMEM((toks, cols), bf16),
+            pltpu.VMEM((full, all_toks, WIDE), bf16),
+            pltpu.VMEM((n_b - full, all_toks, WIDE // 2), bf16),
+            pltpu.VMEM((n_ctx, rows, feats), bf16),
+            pltpu.VMEM((n_ctx, n_tp, rows, feats), bf16),
+            pltpu.VMEM((n_ctx, n_tp, rows, feats), bf16),
+            pltpu.VMEM((feats, all_toks), bf16),
+            pltpu.VMEM((feats, all_toks - 2 * toks), bf16),
+            pltpu.VMEM((n_d, n_tp, rows, d_tile), bf16),
+            pltpu.VMEM((n_d, 2, rows, d_tile), bf16),
+            pltpu.VMEM((n_d, rows, d_tile), bf16),
+            pltpu.VMEM((n_d, rows, d_tile), bf16),
+            pltpu.VMEM((max(full - RAW, 1), feats, WIDE), bf16),
+            pltpu.VMEM((max(full - RAW, 1), feats, WIDE), bf16),
+            pltpu.VMEM((n_b - full, feats, WIDE // 2), bf16),
+            pltpu.VMEM((n_b - full, feats, WIDE // 2), bf16),
+            dma((3,)),
+            dma((2,)),
+            dma((n_b,)),
+            dma((11,)),
+            dma((2, n_ctx)),
+            dma((2, n_ctx)),
+            dma((2, n_ctx // 2)),
+            dma((3, n_b)),
+            dma((n_b,)),
+            dma((n_d,)),
+            dma((n_d,)),
+            dma((n_b,)),
+        ],
+        compiler_params=pltpu.CompilerParams(
+            collective_id=0, has_side_effects=True, vmem_limit_bytes=67_043_328 - outs - 8192
+        ),
+    )(act_codes, scale_exps.T, weight, grad_out)
+
+
+def body(act_codes, scale_exps, weight, grad_out):
+    line, square = lax.axis_size("ctx") // 2, lax.axis_size("tp")
+    if line == 4 and square == 4 and grad_out.shape[1] % WIDE == 0:
+        return square_body(act_codes, scale_exps, weight, grad_out)
+    return line_body(act_codes, scale_exps, weight, grad_out)
+
+
 def solution(mesh):
     placed = (P(("ctx", "tp"), None), P(("ctx", "tp"), None), P(None, "tp"), P("ctx", "tp"))
     return jax.shard_map(

time: 73 us -> 63.4 us (0.87)
  Pallas kernels: 69.6 us -> 60.1 us
    pallas_call x1, Pallas kernels: 69.6 us -> 60.1 us  [square_body(): pl.pallas_call(functools.partial(square_kernel, n_ctx, n_tp, all_toks), o...]
where the time goes in v2:
time: 63.4 us; the launch traced here: 63.2 us
  Pallas kernels  60.1 us (95%)
  local copies, waits for them, and re-layouts  2.46 us (4%)
  between operations  0.64 us (1%)
    pallas_call x1, Pallas kernels, square_body(): pl.pallas_call(functools.partial(square_kernel, n_ctx, n_tp, all_toks), o...  60.1 us
    unnamed x2, local copies, waits for them, and re-layouts  2.46 us

profile of v2, /device:TPU:0, one launch (start us, length us, event | category | flops | bytes accessed | tf_op | source)
XLA Modules:
  0.0 63.2 jit_solution(13323836412541689011)
XLA Ops:
  0.6 60.1 %shard_map.59 = (bf16[64,4096]{1,0:T(8,128)(2,1)S(1)}, f32[512,1536]{1,0:T(8,128)S(1)}) custom-call(bf16[64,4096]{1,0:T(8,128)(2,1)} %codes_hbm.1, s32[32,64]{1,0:T(8,128)} %bitcast.1, bf16[4096,1536]{1,0:T(8,128)(2,1)} %weight_ref.1, bf16[256,1536]{1,0:T(8,128)(2,1)} %grads_ref.1), custom_call_target="tpu_custom_call" | custom-call | tf_op jit(solution)/shard_map/pallas_call | solution.py:940
  60.7 0.8 %copy.8 = bf16[64,4096]{1,0:T(8,128)(2,1)} copy(bf16[64,4096]{1,0:T(8,128)(2,1)S(1)} %get-tuple-element.2) | data formatting | bytes 1048576
  61.5 1.7 %copy.9 = f32[512,1536]{1,0:T(8,128)} copy(f32[512,1536]{1,0:T(8,128)S(1)} %get-tuple-element.3) | data formatting | bytes 6291456

commit v3 on v2

--- a/solution.py
+++ b/solution.py
@@ -384,7 +384,7 @@
     )(act_codes, scale_exps.T, weight, grad_out)
 
 
-RAW = 2
+RAW = 1
 WIDE = 256
 
 
@@ -406,7 +406,7 @@
     gin_ref, gw_ref,
     codes_ref, exps_ref, w_buf, g_own, g_wide, g_slim, a_send, a_buf, p_buf, a_t, p_t,
     part, recv1, total1, recv2, sums_out, sums_in, slim_out, slim_in,
-    in_sem, w_sem, g_sem, s_sem, line_sem, near_sem, rest_sem, g_rsem, mate_sem,
+    in_sem, w_sem, s_sem, line_sem, near_sem, rest_sem, g_rsem, mate_sem,
     one_sem, two_sem, sum_sem,
 ):
     me = lax.axis_index("ctx")
@@ -450,7 +450,7 @@
     def load_g(b):
         start, size = blocks[b]
         return pltpu.make_async_copy(
-            grads_ref.at[:, pl.ds(start, size)], g_piece(me, b), g_sem.at[b]
+            grads_ref.at[:, pl.ds(start, size)], g_piece(me, b), in_sem.at[3]
         )
 
     load_codes = pltpu.make_async_copy(codes_hbm, codes_ref, in_sem.at[0])
@@ -458,8 +458,8 @@
     load_own = pltpu.make_async_copy(grads_ref, g_own, in_sem.at[2])
     load_codes.start()
     load_exps.start()
-    load_g(0).start()
-    load_g(1).start()
+    for b in range(n_b):
+        load_g(b).start()
 
     barrier = pltpu.get_barrier_semaphore()
     for r in range(1, n_ctx):
@@ -472,10 +472,7 @@
         )
     load_exps.wait()
     load_codes.wait()
-    load_own.start()
     load_w(0).start()
-    for b in range(2, n_b):
-        load_g(b).start()
     load_w(1).start()
     powers = jnp.exp2(exps_ref[...].astype(jnp.float32)).T
     for b in range(width // block):
@@ -485,6 +482,8 @@
         a_send[owner, :, place : place + block] = value.astype(jnp.bfloat16)
     a_buf[me, tp] = a_send[me]
     p_buf[me, tp] = a_send[2 * (z_mid + z_end - z) + core]
+    pltpu.make_async_copy(grads_ref, g_own, in_sem.at[3]).wait()
+    load_own.start()
     pl.semaphore_wait(barrier, n_ctx + n_tp - 2)
 
     def program(is_mid):
@@ -511,6 +510,8 @@
                     ref = recv1.at[pl.ds(0, n // 2)]
                 elif n <= n_d:
                     ref = recv2.at[pl.ds(0, n)]
+                elif n % 3 == 0 and n // 3 <= n_d:
+                    ref = part.at[pl.ds(0, n // 3), pl.ds(0, 3)]
                 else:
                     ref = a_buf.at[pl.ds(0, n // n_tp)]
                 assert math.prod(ref.shape) == n * unit
@@ -579,7 +580,6 @@
         FROM_SIDE, FROM_MID, FROM_END = 0, 1, 2
 
         def g_mine(b):
-            load_g(b).wait()
             g_send(5, me, b, g_rsem.at[FROM_MID if is_mid else FROM_SIDE, b], inward)
             if is_mid and b < RAW:
                 g_send(6, me, b, g_rsem.at[FROM_SIDE, b], outward)
@@ -657,7 +657,7 @@
             for half in halves:
                 rhs = g_at(b)[pl.ds(first, (n_line - 1) * chip)]
                 out_at(b)[half] = dot(p_t[half], rhs).astype(jnp.bfloat16)
-                send(10, out_at(b).at[half], in_at(b).at[half], sum_sem.at[b], (outward, tp))
+                send(10, out_at(b).at[half], in_at(b).at[half], sum_sem.at[b - RAW], (outward, tp))
 
         def own_block(b):
             here = pl.ds(pl.multiple_of(z_end * chip, chip), chip)
@@ -665,249 +665,248 @@
                 gw_ref[half, cols(b)] = dot(a_t[half, here], g_at(b)[here])
 
         def add_block(b):
-            landed(in_at(b), sum_sem.at[b])
+            landed(in_at(b), sum_sem.at[b - RAW])
             gw_ref[:, cols(b)] = (gw_ref[:, cols(b)] + in_at(b)[...].astype(jnp.float32)) * scale
 
         if is_mid:
-            g_mine(7)
-            g_mine(3)
             for c in range(2):
                 act_send(2 * z_far_end + c, 2 * z_far_mid + c, ends)
             g_mine(1)
+            g_mine(0)
+            g_mine(3)
             pass_end(me)
             act_send(2 * z_end + 1 - core, mate, ends)
             spread(ends, me)
+            spread(acts, me)
             act_send(mate, mate, acts)
-            spread(acts, me)
             piece(0)
             piece(1)
+            arrive(ends, mate)
             arrive(acts, mate)
-            arrive(ends, mate)
             piece(2)
             piece(3)
             piece(4)
+            arrive(ends, 2 * z_far_mid + core)
             piece(5)
-            g_take(z_far_mid, FROM_MID, 7)
+            piece(6)
             relay(ends, me)
-            piece(6)
+            arrive(ends, 2 * z_far_mid + 1 - core)
+            g_take(z_end, FROM_SIDE, 1)
             piece(7)
+            relay(acts, me)
+            relay(ends, mate)
+            arrive(ends, 2 * z_far_end + core)
+            relay(acts, mate)
+            relay(ends, 2 * z_far_mid + core)
+            g_take(z_far_mid, FROM_MID, 1)
+            arrive(ends, 2 * z_far_end + 1 - core)
+            relay(ends, 2 * z_far_mid + 1 - core)
+            relay(ends, 2 * z_far_end + core)
+            g_take(z_far_mid, FROM_MID, 0)
             g_take(z_far_mid, FROM_MID, 3)
-            relay(acts, me)
-            arrive(ends, 2 * z_far_mid + core)
-            relay(acts, mate)
-            arrive(ends, 2 * z_far_mid + 1 - core)
-            relay(ends, mate)
+            turn(ends, z_mid)
             g_take(z_end, FROM_SIDE, 0)
-            g_mine(0)
+            part_one(0)
+            relay(ends, 2 * z_far_end + 1 - core)
+            turn(acts, z_mid)
+            g_take(z_far_end, FROM_END, 1)
             g_take(z_end, FROM_SIDE, 2)
             g_mine(2)
-            relay(ends, 2 * z_far_mid + core)
-            g_take(z_far_mid, FROM_MID, 1)
-            relay(ends, 2 * z_far_mid + 1 - core)
-            turn(acts, z_mid)
-            part_one(0)
-            arrive(ends, 2 * z_far_end + core)
-            turn(ends, z_mid)
+            g_mates(n_line, 1)
+            part_one(1)
             turn(ends, z_far_mid)
-            arrive(ends, 2 * z_far_end + 1 - core)
             g_take(z_far_end, FROM_END, 0)
             part_two(0)
-            relay(ends, 2 * z_far_end + core)
-            part_one(1)
-            part_one(2)
-            g_take(z_far_mid, FROM_MID, 0)
-            part_one(3)
+            turn(ends, z_far_end)
+            g_mates(n_line, 0)
             g_take(z_end, FROM_SIDE, 3)
+            for c in range(2):
+                act_send(2 * z_far_mid + c, 2 * z_far_mid + c, acts)
+            sum_block(1)
+            g_take(z_far_end, FROM_END, 2)
+            part_two(1)
+            g_take(z_far_mid, FROM_MID, 2)
+            g_take(z_end, FROM_SIDE, 4)
             g_mine(4)
             g_mine(5)
-            relay(ends, 2 * z_far_end + 1 - core)
-            part_one(4)
-            g_mates(n_line, 0)
             g_take(z_end, FROM_SIDE, 5)
-            g_take(z_end, FROM_SIDE, 4)
-            part_sum(0)
-            part_one(5)
-            g_take(z_far_end, FROM_END, 2)
-            part_one(6)
-            part_two(1)
-            turn(ends, z_far_end)
-            g_take(z_far_mid, FROM_MID, 2)
-            g_take(z_end, FROM_SIDE, 6)
             g_mine(6)
-            for c in range(2):
-                act_send(2 * z_far_mid + c, 2 * z_far_mid + c, acts)
-            part_two(2)
+            part_one(2)
+            part_one(3)
             g_mates(n_line, 2)
             sum_block(2)
             g_take(z_far_end, FROM_END, 3)
-            part_two(3)
-            part_sum(1)
-            g_take(z_far_mid, FROM_MID, 4)
+            part_one(4)
+            part_one(5)
             g_mates(n_line, 3)
             sum_block(3)
-            g_take(z_far_mid, FROM_MID, 5)
-            part_sum(2)
+            arrive(acts, 2 * z_far_mid + core)
+            arrive(acts, 2 * z_far_end + core)
+            part_two(2)
+            part_two(3)
+            arrive(acts, 2 * z_far_mid + 1 - core)
+            arrive(acts, 2 * z_far_end + 1 - core)
+            g_take(z_far_end, FROM_END, 4)
+            g_take(z_end, FROM_SIDE, 6)
+            g_mine(7)
+            g_take(z_end, FROM_SIDE, 7)
+            g_mine(8)
+            g_take(z_end, FROM_SIDE, 8)
             part_two(4)
-            g_take(z_far_end, FROM_END, 5)
-            g_take(z_end, FROM_SIDE, 7)
-            g_take(z_end, FROM_SIDE, 1)
-            g_take(z_end, FROM_SIDE, 8)
-            g_mine(8)
+            part_one(6)
             part_one(7)
-            part_sum(3)
-            part_two(5)
-            g_mates(n_line, 5)
-            g_take(z_far_end, FROM_END, 4)
+            g_take(z_far_mid, FROM_MID, 4)
             g_mates(n_line, 4)
             sum_block(4)
-            part_two(6)
-            part_sum(4)
+            g_take(z_far_mid, FROM_MID, 5)
+            part_two(5)
+            g_take(z_far_end, FROM_END, 5)
+            relay(acts, 2 * z_far_mid + core)
+            g_mates(n_line, 5)
             sum_block(5)
+            g_take(z_far_mid, FROM_MID, 6)
+            relay(acts, 2 * z_far_end + core)
             g_take(z_far_end, FROM_END, 6)
-            part_sum(5)
-            part_two(7)
-            g_take(z_far_mid, FROM_MID, 6)
-            arrive(acts, 2 * z_far_end + core)
-            part_sum(6)
+            turn_whole(z_end)
+            relay(acts, 2 * z_far_mid + 1 - core)
             g_mates(n_line, 6)
             sum_block(6)
-            arrive(acts, 2 * z_far_mid + core)
-            part_sum(7)
-            arrive(acts, 2 * z_far_end + 1 - core)
-            arrive(acts, 2 * z_far_mid + 1 - core)
-            turn_whole(z_end)
-            relay(acts, 2 * z_far_end + core)
+            g_take(z_far_mid, FROM_MID, 7)
+            relay(acts, 2 * z_far_end + 1 - core)
             g_take(z_far_end, FROM_END, 7)
-            relay(acts, 2 * z_far_mid + core)
             g_mates(n_line, 7)
             sum_block(7)
-            relay(acts, 2 * z_far_end + 1 - core)
-            g_take(z_far_end, FROM_END, 1)
-            relay(acts, 2 * z_far_mid + 1 - core)
-            g_mates(n_line, 1)
+            g_take(z_far_mid, FROM_MID, 8)
+            part_two(6)
             g_take(z_far_end, FROM_END, 8)
-            g_take(z_far_mid, FROM_MID, 8)
-            turn(acts, z_far_end)
             g_mates(n_line, 8)
             sum_block(8)
+            part_two(7)
             turn(acts, z_far_mid)
+            turn(acts, z_far_end)
             whole_block(0)
             whole_block(1)
             whole_block(2)
             whole_pair(3)
             whole_pair(5)
             whole_pair(7)
+            part_sum(0)
+            part_sum(1)
+            part_sum(2)
+            part_sum(3)
+            part_sum(4)
+            part_sum(5)
+            part_sum(6)
+            part_sum(7)
         else:
             act_send(2 * z_mid + 1 - core, mate, ends)
             spread(ends, me)
             act_send(mate, mate, acts)
-            g_mine(4)
-            g_mine(2)
-            g_mine(0)
-            pass_back(me, tp)
+            g_mine(1)
             for c in range(2):
                 act_send(2 * z_far_end + c, 2 * z_far_mid + c, ends)
+            pass_back(me, tp)
+            g_mine(0)
+            g_mine(2)
             spread(acts, me)
             piece(0)
+            piece(1)
             arrive(ends, mate)
             arrive(acts, mate)
-            piece(1)
             part_one(0)
             piece(2)
             piece(3)
             piece(4)
             piece(5)
+            piece(6)
             relay(ends, me)
-            piece(6)
+            g_take(z_mid, FROM_SIDE, 0)
             piece(7)
+            part_one(1)
             relay(acts, me)
-            g_take(z_mid, FROM_SIDE, 1)
+            part_one(2)
+            arrive(acts, 2 * z_mid + core)
             relay(ends, mate)
-            arrive(acts, 2 * z_mid + core)
-            part_one(1)
+            arrive(acts, 2 * z_mid + 1 - core)
+            part_one(3)
             relay(acts, mate)
-            arrive(acts, 2 * z_mid + 1 - core)
-            part_one(2)
             arrive(acts, 2 * z_far_mid + core)
+            arrive(acts, 2 * z_far_mid + 1 - core)
+            part_one(4)
+            part_one(5)
             part_two(0)
-            arrive(acts, 2 * z_far_mid + 1 - core)
+            arrive(acts, 2 * z_far_end + core)
+            part_one(6)
             gathered(ends, z_end)
-            pass_back(mate, next_)
-            pass_back(mate, tp)
+            pass_back(me, diag)
+            g_mine(7)
             g_mine(3)
             g_mine(5)
             g_mine(8)
-            pass_back(me, next_)
-            g_mine(6)
-            g_mine(1)
-            pass_back(me, diag)
-            g_mine(7)
-            pass_back(mate, near)
-            pass_back(mate, diag)
+            g_mine(4)
+            pass_back(me, near)
             for c in range(2):
                 act_send(2 * z_far_mid + c, 2 * z_far_mid + c, acts)
-            pass_back(me, near)
-            relay(acts, 2 * z_mid + core)
-            part_one(3)
-            g_take(z_mid, FROM_SIDE, 0)
+            g_mine(6)
+            pass_back(mate, near)
+            pass_back(me, next_)
+            pass_back(mate, diag)
+            pass_back(mate, next_)
+            pass_back(mate, tp)
+            arrive(acts, 2 * z_far_end + 1 - core)
             part_two(1)
+            part_one(7)
             turn(acts, z_end)
+            g_mates(1, 1)
+            own_block(1)
             g_mates(1, 2)
             own_block(2)
             g_mates(1, 3)
             own_block(3)
+            g_take(z_far_mid, FROM_MID, 0)
             g_mates(1, 4)
             own_block(4)
             g_mates(1, 5)
             own_block(5)
+            relay(acts, 2 * z_mid + core)
             g_mates(1, 6)
             own_block(6)
-            relay(acts, 2 * z_mid + 1 - core)
             g_mates(1, 7)
             own_block(7)
             g_mates(1, 8)
             own_block(8)
-            g_take(z_far_mid, FROM_MID, 1)
-            arrive(acts, 2 * z_far_end + core)
             part_two(2)
+            relay(acts, 2 * z_mid + 1 - core)
             part_sum(0)
-            arrive(acts, 2 * z_far_end + 1 - core)
+            part_two(3)
             relay(acts, 2 * z_far_mid + core)
+            g_take(z_far_end, FROM_END, 0)
             relay(acts, 2 * z_far_mid + 1 - core)
-            part_one(4)
-            part_one(5)
-            part_one(6)
-            g_take(z_far_end, FROM_END, 0)
             part_sum(1)
-            part_one(7)
-            part_two(3)
-            turn(acts, z_mid)
-            g_take(z_far_mid, FROM_MID, 0)
-            relay(acts, 2 * z_far_end + core)
             g_mates(n_line, 0)
-            relay(acts, 2 * z_far_end + 1 - core)
             part_sum(2)
             part_two(4)
+            turn(acts, z_mid)
+            add_block(1)
+            part_sum(3)
+            part_two(5)
+            relay(acts, 2 * z_far_end + core)
             turn(acts, z_far_mid)
-            part_two(5)
-            part_sum(3)
+            part_sum(4)
+            part_two(6)
             add_block(2)
-            part_two(6)
+            relay(acts, 2 * z_far_end + 1 - core)
+            part_sum(5)
+            add_block(3)
+            part_two(7)
+            part_sum(6)
             turn(acts, z_far_end)
             whole_block(0)
-            part_sum(4)
-            add_block(3)
-            part_two(7)
-            part_sum(5)
-            part_sum(6)
             add_block(4)
             part_sum(7)
             add_block(5)
             add_block(6)
             add_block(7)
-            g_take(z_far_end, FROM_END, 1)
-            g_mates(n_line, 1)
-            whole_block(1)
             add_block(8)
         all_sent()
 
@@ -937,7 +936,7 @@
     hbm = pl.BlockSpec(memory_space=pltpu.HBM)
     bf16 = jnp.bfloat16
     outs = rows * width * 2 + feats * cols * 4
-    return pl.pallas_call(
+    gin, gw = pl.pallas_call(
         functools.partial(square_kernel, n_ctx, n_tp, all_toks),
         out_shape=(
             pltpu.VMEM((rows, width), bf16),
@@ -965,9 +964,8 @@
             pltpu.VMEM((max(full - RAW, 1), feats, WIDE), bf16),
             pltpu.VMEM((n_b - full, feats, WIDE // 2), bf16),
             pltpu.VMEM((n_b - full, feats, WIDE // 2), bf16),
-            dma((3,)),
+            dma((4,)),
             dma((2,)),
-            dma((n_b,)),
             dma((11,)),
             dma((2, n_ctx)),
             dma((2, n_ctx)),
@@ -976,12 +974,33 @@
             dma((n_b,)),
             dma((n_d,)),
             dma((n_d,)),
-            dma((n_b,)),
+            dma((n_b - RAW,)),
         ],
         compiler_params=pltpu.CompilerParams(
             collective_id=0, has_side_effects=True, vmem_limit_bytes=67_043_328 - outs - 8192
         ),
     )(act_codes, scale_exps.T, weight, grad_out)
+    return pl.pallas_call(
+        store_kernel,
+        out_shape=(
+            jax.ShapeDtypeStruct(gin.shape, gin.dtype), jax.ShapeDtypeStruct(gw.shape, gw.dtype)
+        ),
+        in_specs=[vmem, vmem],
+        out_specs=(hbm, hbm),
+        scratch_shapes=[dma((2,))],
+        compiler_params=pltpu.CompilerParams(vmem_limit_bytes=1 << 20),
+    )(gin, gw)
+
+
+def store_kernel(gin_ref, gw_ref, gin_out, gw_out, sem):
+    copies = [
+        pltpu.make_async_copy(gw_ref, gw_out, sem.at[0]),
+        pltpu.make_async_copy(gin_ref, gin_out, sem.at[1]),
+    ]
+    for copy in copies:
+        copy.start()
+    for copy in copies:
+        copy.wait()
 
 
 def body(act_codes, scale_exps, weight, grad_out):

time: 63.4 us -> 62.4 us (0.984)
  local copies, waits for them, and re-layouts: 2.46 us -> 0 us
  Pallas kernels: 60.1 us -> 61.4 us
    unnamed x2 -> x0, local copies, waits for them, and re-layouts: 2.46 us -> none
    pallas_call x0 -> x1, Pallas kernels: none -> 1.85 us  [square_body(): pl.pallas_call(store_kernel, out_shape=(jax.ShapeDtypeStruct(gin.shape, g...]
where the time goes in v3:
time: 62.4 us; the launch traced here: 62.2 us
  Pallas kernels  61.4 us (98%)
  between operations  0.8 us (1%)
    pallas_call x1, Pallas kernels, square_body(): pl.pallas_call(functools.partial(square_kernel, n_ctx, n_tp, all_toks), o...  59.6 us
    pallas_call x1, Pallas kernels, square_body(): pl.pallas_call(store_kernel, out_shape=(jax.ShapeDtypeStruct(gin.shape, g...  1.85 us

profile of v3, /device:TPU:0, one launch (start us, length us, event | category | flops | bytes accessed | tf_op | source)
XLA Modules:
  0.0 62.2 jit_solution(9767240053664219331)
XLA Ops:
  0.6 59.6 %shard_map.59 = (bf16[64,4096]{1,0:T(8,128)(2,1)S(1)}, f32[512,1536]{1,0:T(8,128)S(1)}) custom-call(bf16[64,4096]{1,0:T(8,128)(2,1)} %codes_hbm.1, s32[32,64]{1,0:T(8,128)} %bitcast.1, bf16[4096,1536]{1,0:T(8,128)(2,1)} %weight_ref.1, bf16[256,1536]{1,0:T(8,128)(2,1)} %grads_ref.1), custom_call_target="tpu_custom_call" | custom-call | tf_op jit(solution)/shard_map/pallas_call | solution.py:939
  60.2 1.8 %shard_map.60 = (bf16[64,4096]{1,0:T(8,128)(2,1)}, f32[512,1536]{1,0:T(8,128)}) custom-call(bf16[64,4096]{1,0:T(8,128)(2,1)S(1)} %get-tuple-element.4.gin_ref, f32[512,1536]{1,0:T(8,128)S(1)} %get-tuple-element.5.gw_ref), custom_call_target="tpu_custom_call" | custom-call | tf_op jit(solution)/shard_map/pallas_call | solution.py:983

commit v4 on v3

--- a/solution.py
+++ b/solution.py
@@ -645,6 +645,26 @@
             for half in halves:
                 rhs = jnp.concatenate([g_at(b)[...], g_at(b + 1)[...]], axis=1)
                 gw_ref[half, start : start + 2 * size] = dot(a_t[half], rhs) * scale
+
+        def tokens_of(near_side):
+            first = (side if near_side else 1 - side) * 2 * chip
+            return pl.ds(pl.multiple_of(first, 2 * chip), 2 * chip)
+
+        def rhs_of(b, toks_at):
+            if b < full:
+                return g_at(b)[toks_at]
+            return jnp.concatenate([g_at(b)[toks_at], g_at(b + 1)[toks_at]], axis=1)
+
+        def early_block(b):
+            start, toks_at = blocks[b][0], tokens_of(True)
+            for half in halves:
+                gw_ref[half, start : start + WIDE] = dot(a_t[half, toks_at], rhs_of(b, toks_at))
+
+        def late_block(b):
+            start, toks_at = blocks[b][0], tokens_of(False)
+            for half in halves:
+                term = dot(a_t[half, toks_at], rhs_of(b, toks_at))
+                gw_ref[half, start : start + WIDE] = (gw_ref[half, start : start + WIDE] + term) * scale
 
         def out_at(b):
             return sums_out.at[b - RAW] if b < full else slim_out.at[b - full]
@@ -759,36 +779,41 @@
             g_mates(n_line, 4)
             sum_block(4)
             g_take(z_far_mid, FROM_MID, 5)
+            g_take(z_far_end, FROM_END, 5)
             part_two(5)
-            g_take(z_far_end, FROM_END, 5)
-            relay(acts, 2 * z_far_mid + core)
             g_mates(n_line, 5)
             sum_block(5)
+            relay(acts, 2 * z_far_mid + core)
             g_take(z_far_mid, FROM_MID, 6)
+            g_take(z_far_end, FROM_END, 6)
             relay(acts, 2 * z_far_end + core)
-            g_take(z_far_end, FROM_END, 6)
             turn_whole(z_end)
-            relay(acts, 2 * z_far_mid + 1 - core)
             g_mates(n_line, 6)
             sum_block(6)
+            relay(acts, 2 * z_far_mid + 1 - core)
             g_take(z_far_mid, FROM_MID, 7)
+            g_take(z_far_end, FROM_END, 7)
             relay(acts, 2 * z_far_end + 1 - core)
-            g_take(z_far_end, FROM_END, 7)
+            early_block(0)
             g_mates(n_line, 7)
             sum_block(7)
             g_take(z_far_mid, FROM_MID, 8)
-            part_two(6)
             g_take(z_far_end, FROM_END, 8)
+            early_block(1)
             g_mates(n_line, 8)
             sum_block(8)
-            part_two(7)
+            early_block(2)
+            early_block(3)
+            early_block(5)
+            part_two(6)
             turn(acts, z_far_mid)
             turn(acts, z_far_end)
-            whole_block(0)
-            whole_block(1)
-            whole_block(2)
-            whole_pair(3)
-            whole_pair(5)
+            late_block(0)
+            late_block(1)
+            part_two(7)
+            late_block(2)
+            late_block(3)
+            late_block(5)
             whole_pair(7)
             part_sum(0)
             part_sum(1)

time: 62.4 us -> 62.3 us (level)
  no operation moved by 1% of the time
where the time goes in v4:
time: 62.3 us; the launch traced here: 62.2 us
  Pallas kernels  61.4 us (99%)
  between operations  0.8 us (1%)
    pallas_call x1, Pallas kernels, square_body(): pl.pallas_call(functools.partial(square_kernel, n_ctx, n_tp, all_toks), o...  59.5 us
    pallas_call x1, Pallas kernels, square_body(): pl.pallas_call(store_kernel, out_shape=(jax.ShapeDtypeStruct(gin.shape, g...  1.85 us

profile of v4, /device:TPU:0, one launch (start us, length us, event | category | flops | bytes accessed | tf_op | source)
XLA Modules:
  0.0 62.2 jit_solution(14981995199779436927)
XLA Ops:
  0.6 59.5 %shard_map.59 = (bf16[64,4096]{1,0:T(8,128)(2,1)S(1)}, f32[512,1536]{1,0:T(8,128)S(1)}) custom-call(bf16[64,4096]{1,0:T(8,128)(2,1)} %codes_hbm.1, s32[32,64]{1,0:T(8,128)} %bitcast.1, bf16[4096,1536]{1,0:T(8,128)(2,1)} %weight_ref.1, bf16[256,1536]{1,0:T(8,128)(2,1)} %grads_ref.1), custom_call_target="tpu_custom_call" | custom-call | tf_op jit(solution)/shard_map/pallas_call | solution.py:964
  60.2 1.8 %shard_map.60 = (bf16[64,4096]{1,0:T(8,128)(2,1)}, f32[512,1536]{1,0:T(8,128)}) custom-call(bf16[64,4096]{1,0:T(8,128)(2,1)S(1)} %get-tuple-element.4.gin_ref, f32[512,1536]{1,0:T(8,128)S(1)} %get-tuple-element.5.gw_ref), custom_call_target="tpu_custom_call" | custom-call | tf_op jit(solution)/shard_map/pallas_call | solution.py:1008

commit v5 on v4

--- a/solution.py
+++ b/solution.py
@@ -462,14 +462,25 @@
         load_g(b).start()
 
     barrier = pltpu.get_barrier_semaphore()
-    for r in range(1, n_ctx):
-        pl.semaphore_signal(
-            barrier, inc=1, device_id=(lax.rem(me + r, n_ctx), tp), device_id_type=MESH
-        )
-    for r in range(1, n_tp):
-        pl.semaphore_signal(
-            barrier, inc=1, device_id=(me, lax.rem(tp + r, n_tp)), device_id_type=MESH
-        )
+    end_chip = z != z_mid
+
+    def greet(ctx, square):
+        pl.semaphore_signal(barrier, inc=1, device_id=(ctx, square), device_id_type=MESH)
+
+    greet(mate, tp)
+    greet(me, near)
+    greet(me, next_)
+
+    @pl.when(end_chip)
+    def _():
+        greet(2 * z_mid + core, tp)
+
+    @pl.when(jnp.logical_not(end_chip))
+    def _():
+        for zz in (z_end, z_far_mid, z_far_end):
+            for c in range(2):
+                greet(2 * zz + c, tp)
+
     load_exps.wait()
     load_codes.wait()
     load_w(0).start()
@@ -484,7 +495,13 @@
     p_buf[me, tp] = a_send[2 * (z_mid + z_end - z) + core]
     pltpu.make_async_copy(grads_ref, g_own, in_sem.at[3]).wait()
     load_own.start()
-    pl.semaphore_wait(barrier, n_ctx + n_tp - 2)
+    @pl.when(end_chip)
+    def _():
+        pl.semaphore_wait(barrier, 7)
+
+    @pl.when(jnp.logical_not(end_chip))
+    def _():
+        pl.semaphore_wait(barrier, 6)
 
     def program(is_mid):
         sent = {}

time: 62.3 us -> 61.5 us (0.987)
  Pallas kernels: 61.4 us -> 60.5 us
    pallas_call x1, Pallas kernels: 59.5 us -> 58.6 us  [square_body(): pl.pallas_call(functools.partial(square_kernel, n_ctx, n_tp, all_toks), o...]
where the time goes in v5:
time: 61.5 us; the launch traced here: 61.3 us
  Pallas kernels  60.5 us (98%)
  between operations  0.8 us (1%)
    pallas_call x1, Pallas kernels, square_body(): pl.pallas_call(functools.partial(square_kernel, n_ctx, n_tp, all_toks), o...  58.6 us
    pallas_call x1, Pallas kernels, square_body(): pl.pallas_call(store_kernel, out_shape=(jax.ShapeDtypeStruct(gin.shape, g...  1.85 us

profile of v5, /device:TPU:0, one launch (start us, length us, event | category | flops | bytes accessed | tf_op | source)
XLA Modules:
  0.0 61.3 jit_solution(9041190442056137862)
XLA Ops:
  0.6 58.6 %shard_map.59 = (bf16[64,4096]{1,0:T(8,128)(2,1)S(1)}, f32[512,1536]{1,0:T(8,128)S(1)}) custom-call(bf16[64,4096]{1,0:T(8,128)(2,1)} %codes_hbm.1, s32[32,64]{1,0:T(8,128)} %bitcast.1, bf16[4096,1536]{1,0:T(8,128)(2,1)} %weight_ref.1, bf16[256,1536]{1,0:T(8,128)(2,1)} %grads_ref.1), custom_call_target="tpu_custom_call" | custom-call | tf_op jit(solution)/shard_map/pallas_call | solution.py:981
  59.3 1.8 %shard_map.60 = (bf16[64,4096]{1,0:T(8,128)(2,1)}, f32[512,1536]{1,0:T(8,128)}) custom-call(bf16[64,4096]{1,0:T(8,128)(2,1)S(1)} %get-tuple-element.4.gin_ref, f32[512,1536]{1,0:T(8,128)S(1)} %get-tuple-element.5.gw_ref), custom_call_target="tpu_custom_call" | custom-call | tf_op jit(solution)/shard_map/pallas_call | solution.py:1025
